TPU v7x, 32 devices: a whole 2x2x4 slice. The times are simulated.
32 devices in a mesh: expert: 8 (over z, x), pair: 4 (over y, core).
Axes of the slice: x: 2, y: 2, z: 4, core: 2. Of those that a mesh axis runs over, the one named last changes fastest.
Arguments:
- tokens: bfloat16 [12288, 2048], P(('expert', 'pair')), may hold values from -6 to 6
- token_ids: int32 [12288], P(('expert', 'pair')), may hold values from 0 to 8191
- table: int32 [8192], replicated, may hold values from 0 to 15
- w_in: bfloat16 [16, 2048, 2048], P('expert', None, 'pair'), may hold values from -0.125 to 0.125
- w_out: bfloat16 [16, 2048, 2048], P('expert', 'pair'), may hold values from -0.125 to 0.125
Outputs:
- mixed: bfloat16 [12288, 2048], P(('expert', 'pair'))
All inputs are finite; a program needn't handle non-finite values.
Results may differ from a plain program's by a relative error of at most 0.0085.
Values may be sent and summed in bfloat16 or wider, within the bound.
A program may use at most 192 MiB of HBM per device.

v0:
```python
import jax
import jax.numpy as jnp
from jax import lax
from jax.sharding import PartitionSpec as P


def on_device(tokens, token_ids, table, w_in, w_out):
    groups = lax.axis_size("expert")
    exp_local = w_in.shape[0]
    experts = groups * exp_local
    tok_rows, width = tokens.shape
    slots = max(2, 2 * tok_rows // experts)
    quarter = w_out.shape[1]
    chosen = jnp.take(table, token_ids, axis=0)
    expert_hot = (chosen[:, None] == jnp.arange(experts, dtype=jnp.int32)[None, :]).astype(
        jnp.int32
    )
    earlier = jnp.cumsum(expert_hot, axis=0) - expert_hot
    rank_tok = jnp.sum(earlier * expert_hot, axis=1)
    kept = rank_tok < slots
    column = (chosen // exp_local * slots + rank_tok) * exp_local + chosen % exp_local
    placer = (
        (column[:, None] == jnp.arange(experts * slots, dtype=jnp.int32)[None, :]) & kept[:, None]
    ).astype(jnp.bfloat16)
    packed = jnp.einsum("ts,td->sd", placer, tokens, preferred_element_type=jnp.float32).astype(
        jnp.bfloat16
    )
    packed = packed.reshape(groups * slots, exp_local, width)
    arrived = lax.all_to_all(packed, "expert", split_axis=0, concat_axis=0, tiled=True)
    rows = arrived.shape[0]
    hidden = jax.nn.relu(
        jnp.einsum(
            "red,edh->reh",
            arrived,
            lax.all_gather(w_in, "pair", axis=2, tiled=True),
            preferred_element_type=jnp.float32,
        )
    ).astype(jnp.bfloat16)
    total = jnp.zeros((rows, exp_local, width), jnp.float32)
    piece = lax.all_gather(w_out, "pair", axis=1, tiled=True)
    for index in range(piece.shape[1] // quarter):
        cols = lax.dynamic_slice_in_dim(hidden, index * quarter, quarter, 2)
        part = jnp.einsum(
            "reh,ehd->red",
            cols,
            piece[:, index * quarter : (index + 1) * quarter],
            preferred_element_type=jnp.float32,
        ).astype(jnp.bfloat16)
        total = total + lax.optimization_barrier(part).astype(jnp.float32)
    result = total.astype(jnp.bfloat16)
    returned = lax.all_to_all(result, "expert", split_axis=0, concat_axis=0, tiled=True)
    flat = returned.reshape(experts * slots, width)
    return jnp.dot(placer, flat, preferred_element_type=jnp.float32).astype(jnp.bfloat16)


def solution(mesh):
    in_specs = (
        P(("expert", "pair"), None),
        P(("expert", "pair")),
        P(),
        P("expert", None, "pair"),
        P("expert", "pair", None),
    )
    out_specs = P(("expert", "pair"), None)
    return jax.shard_map(
        on_device, mesh=mesh, in_specs=in_specs, out_specs=out_specs, check_vma=False
    )
```

profile of v0, /device:TPU:0, one launch (start us, length us, event | category | flops | bytes accessed | tf_op | source)
XLA Modules:
  0.0 337.7 jit_solution(6098488606454812090)
XLA Ops:
  6.5 0.0 copy-start
  6.5 0.0 copy-start.3
  6.5 0.0 all-gather.3.cloned.1.call-start
  6.5 0.7 all-gather.3.cloned.1.call-update
  7.3 0.0 copy-start.2
  7.3 0.0 all-gather.5.cloned.1.call-start
  7.3 0.7 all-gather.5.cloned.1.call-update
  8.0 0.0 copy-done.3
  8.1 0.0 copy-done.2
  8.1 2.5 gather_fusion
  10.6 0.9 reduce-window.6
  11.5 0.2 slice_reduce_fusion
  11.8 0.1 fusion.49
  11.9 0.0 copy-done
  11.9 3.6 %convolution_convert_fusion = bf16[768,2048]{1,0:T(8,128)(2,1)} fusion(bf16[384,2048]{1,0:T(8,128)(2,1)S(1)} %copy-done, s32[384]{0:T(512)S(1)} %fusion.54, pred[384]{0:T(512)(128)(4,1)S(1)} %broadcast_compare_fusion), kind=kOutput, calls=%fused_computation.11 | convolution fusion | flops 1210122240 | bytes 4720512 | tf_op jit(solution)/shard_map/ts,td->sd/dot_general | solution.py:25
  15.5 4.7 %reshape.67 = bf16[384,2,2048]{2,1,0:T(2,128)(2,1)S(1)} reshape(bf16[768,2048]{1,0:T(8,128)(2,1)} %convolution_convert_fusion) | data formatting | bytes 6291456 | tf_op jit(solution)/shard_map/reshape | solution.py:28
  20.2 78.0 %all_to_all.10 = bf16[384,2,2048]{2,1,0:T(2,128)(2,1)} all-to-all(bf16[384,2,2048]{2,1,0:T(2,128)(2,1)S(1)} %reshape.67), channel_id=1, replica_groups=mesh['expert'=8,'pair'=4] {'expert'}, dimensions={0} | all-to-all | bytes 6291456 | tf_op jit(solution)/shard_map/all_to_all | solution.py:29
  98.2 19.3 %all-gather.3.cloned.1.call-done = bf16[2,2048,2048]{2,1,0:T(8,128)(2,1)} async-done(((bf16[2,2048,512]{2,1,0:T(8,128)(2,1)}), bf16[2,2048,2048]{2,1,0:T(8,128)(2,1)}) %all-gather.3.cloned.1.call-update) | async-done | bytes 16777232 | tf_op jit(solution)/shard_map/all_gather | solution.py:35
  117.6 14.0 %fusion.33 = bf16[384,2,2048]{2,0,1:T(8,128)(2,1)S(1)} fusion(bf16[2,2048,2048]{2,1,0:T(8,128)(2,1)} %all-gather.3.cloned.1.call-done, bf16[384,2,2048]{2,1,0:T(2,128)(2,1)} %all_to_all.10), kind=kOutput, calls=%fused_computation.21 | convolution fusion | flops 6445596672 | bytes 23068672 | tf_op jit(solution)/shard_map/red,edh->reh/dot_general | solution.py:32
  131.6 93.5 %all-gather.5.cloned.1.call-done = bf16[2,2048,2048]{2,1,0:T(8,128)(2,1)} async-done(((bf16[2,512,2048]{2,1,0:T(8,128)(2,1)}), bf16[2,2048,2048]{2,1,0:T(8,128)(2,1)}) %all-gather.5.cloned.1.call-update) | async-done | bytes 16777232 | tf_op jit(solution)/shard_map/all_gather | solution.py:40
  225.0 0.0 copy-start.4
  225.0 4.1 %fusion.30 = bf16[384,2,2048]{2,0,1:T(8,128)(2,1)S(1)} fusion(bf16[2,2048,2048]{2,1,0:T(8,128)(2,1)} %all-gather.5.cloned.1.call-done, bf16[384,2,2048]{2,0,1:T(8,128)(2,1)S(1)} %fusion.33), kind=kOutput, calls=%fused_computation.20 | convolution fusion | flops 1612185600 | bytes 8126464 | tf_op jit(solution)/shard_map/reh,ehd->red/dot_general | solution.py:43
  229.2 4.7 %fusion.27 = bf16[384,2,2048]{2,0,1:T(8,128)(2,1)S(1)} fusion(bf16[2,2048,2048]{2,1,0:T(8,128)(2,1)} %all-gather.5.cloned.1.call-done, bf16[384,2,2048]{2,0,1:T(8,128)(2,1)S(1)} %fusion.33), kind=kOutput, calls=%fused_computation.19 | convolution fusion | flops 1612185600 | bytes 8126464 | tf_op jit(solution)/shard_map/reh,ehd->red/dot_general | solution.py:43
  233.9 0.0 copy-done.4
  233.9 1.8 fusion.24
  235.8 1.8 fusion.21
  237.6 3.2 add_convert_fusion
  240.8 3.2 copy.12
  244.1 76.5 %all_to_all.11 = bf16[384,2,2048]{2,1,0:T(2,128)(2,1)} all-to-all(bf16[384,2,2048]{2,1,0:T(2,128)(2,1)S(1)} %copy.12), channel_id=1, replica_groups=mesh['expert'=8,'pair'=4] {'expert'}, dimensions={0} | all-to-all | bytes 6291456 | tf_op jit(solution)/shard_map/all_to_all | solution.py:51
  320.6 0.0 copy-start.1
  320.6 5.8 %reshape.68 = bf16[768,2048]{1,0:T(8,128)(2,1)} reshape(bf16[384,2,2048]{2,1,0:T(2,128)(2,1)} %all_to_all.11) | data formatting | bytes 6291456 | tf_op jit(solution)/shard_map/reshape | solution.py:52
  326.4 4.5 %convolution_convert_fusion.1 = bf16[384,2048]{1,0:T(8,128)(2,1)} fusion(bf16[768,2048]{1,0:T(8,128)(2,1)} %reshape.68, s32[384]{0:T(512)S(1)} %fusion.54, pred[384]{0:T(512)(128)(4,1)S(1)} %broadcast_compare_fusion), kind=kOutput, calls=%fused_computation.22 | convolution fusion | flops 1209335808 | bytes 4720512 | tf_op jit(solution)/shard_map/dot_general | solution.py:53
  330.9 0.0 copy-done.1
  (7 shorter events, 0.1 us)
Async XLA Ops:
  6.5 5.4 %copy-start = (bf16[384,2048]{1,0:T(8,128)(2,1)S(1)}, bf16[384,2048]{1,0:T(8,128)(2,1)}, u32[]{:S(2)}) copy-start(bf16[384,2048]{1,0:T(8,128)(2,1)} %param.5) | copy-start | bytes 4718596
  6.5 1.5 copy-start.3
  6.5 111.0 %all-gather.3.cloned.1.call-start = ((), (), s32[]{:S(2)}) async-start(), calls=%async_computation.2 | async-start | bytes 20971520 | tf_op jit(solution)/shard_map/all_gather | solution.py:35
  7.3 0.8 copy-start.2
  7.3 217.8 %all-gather.5.cloned.1.call-start = ((), (), s32[]{:S(2)}) async-start(), calls=%async_computation.3 | async-start | bytes 20971520 | tf_op jit(solution)/shard_map/all_gather | solution.py:40
  225.0 8.9 %copy-start.4 = (bf16[2,2048,2048]{2,1,0:T(8,128)(2,1)S(1)}, bf16[2,2048,2048]{2,1,0:T(8,128)(2,1)}, u32[]{:S(2)}) copy-start(bf16[2,2048,2048]{2,1,0:T(8,128)(2,1)} %all-gather.5.cloned.1.call-done) | copy-start | bytes 50331652
  320.6 10.3 %copy-start.1 = (bf16[384,2048]{1,0:T(8,128)(2,1)S(1)}, bf16[384,2048]{1,0:T(8,128)(2,1)}, u32[]{:S(2)}) copy-start(bf16[384,2048]{1,0:T(8,128)(2,1)} %param.5) | copy-start | bytes 4718596
Sparse Core Ops, SparseCore 0:
  8.9 108.6 all-gather.2
  119.1 105.8 all-gather.4
where the time goes:
time: 338 us
  blocking collectives  154 us (46%)
  waiting for transfers between devices  114 us (34%)
  matrix products  34.6 us (10%)
  local copies, waits for them, and re-layouts  16.6 us (5%)
  between operations  13.5 us (4%)
  other arithmetic  4.29 us (1%)
    all_gather x1, waiting for transfers between devices, on_device(): piece = lax.all_gather(w_out, 'pair', axis=1, tiled=True)  93.5 us
    all_to_all x1, blocking collectives, on_device(): lax.all_to_all(packed, 'expert', split_axis=0, concat_axis=0, tiled=True)  78 us
    all_to_all x1, blocking collectives, on_device(): lax.all_to_all(result, 'expert', split_axis=0, concat_axis=0, tiled=True)  76.5 us
    all_gather x1, waiting for transfers between devices, on_device(): lax.all_gather(w_in, 'pair', axis=2, tiled=True)  19.3 us
    dot_general x1, matrix products, on_device(): jnp.einsum('red,edh->reh', arrived, lax.all_gather(w_in, 'pair', axis=2,...  14 us
    dot_general x4, matrix products, on_device(): jnp.einsum('reh,ehd->red', cols, piece[:, index * quarter:(index + 1) * q...  12.5 us
  transfers between devices with their start and end apart: 2, of which 2 were waited for; matrix products, arithmetic and copies ran while one was open for 8% of the time, Pallas kernels for 0%

commit v1 on v0

--- a/solution.py
+++ b/solution.py
@@ -1,10 +1,238 @@
+import functools
+
 import jax
 import jax.numpy as jnp
 from jax import lax
+from jax.experimental import pallas as pl
+from jax.experimental.pallas import tpu as pltpu
 from jax.sharding import PartitionSpec as P
 
-
-def on_device(tokens, token_ids, table, w_in, w_out):
+ROWS = 16
+TILE = 256
+MESH = pl.DeviceIdType.MESH
+
+
+def exact_dot(a, b):
+    return jnp.dot(a, b, preferred_element_type=jnp.float32)
+
+
+def layer_kernel(
+    n,
+    packed,
+    w_in,
+    w_out,
+    back,
+    first,
+    second,
+    rows,
+    hidden,
+    part,
+    near,
+    far,
+    own_sem,
+    w_sem,
+    go_sem,
+    come_sem,
+    pair_go,
+    pair_come,
+):
+    chunks = packed.shape[0]
+    per_expert = chunks // w_in.shape[0]
+    me = lax.axis_index("expert")
+    at = lax.axis_index("pair")
+    core = {"pair": at + 1 - 2 * (at % 2)}
+    chip = {"pair": (at + 2) % 4}
+    ahead = [{"expert": (me + j) % n} for j in range(n)]
+    behind = [{"expert": (me + n - j) % n} for j in range(n)]
+
+    w_copies = [
+        pltpu.make_async_copy(w_in, first, w_sem.at[0]),
+        pltpu.make_async_copy(w_out, second, w_sem.at[1]),
+    ]
+    for copy in w_copies:
+        copy.start()
+
+    barrier = pltpu.get_barrier_semaphore()
+    for peer in [core, chip] + ahead[1:]:
+        pl.semaphore_signal(barrier, inc=1, device_id=peer, device_id_type=MESH)
+    pl.semaphore_wait(barrier, n + 1)
+
+    def remote(src, dst, send, recv, peer):
+        copy = pltpu.make_async_remote_copy(
+            src_ref=src,
+            dst_ref=dst,
+            send_sem=send,
+            recv_sem=recv,
+            device_id=peer,
+            device_id_type=MESH,
+        )
+        copy.start()
+        return copy
+
+    sent = []
+    dispatch = []
+    for c in range(chunks):
+        copies = [
+            remote(
+                packed.at[c, pl.ds(j * ROWS, ROWS)],
+                rows.at[c, 0, pl.ds(j * ROWS, ROWS)],
+                go_sem.at[0, c, j],
+                come_sem.at[0, c, j],
+                ahead[j],
+            )
+            for j in range(1, n)
+        ]
+        own = pltpu.make_async_copy(
+            packed.at[c, pl.ds(0, ROWS)], rows.at[c, 0, pl.ds(0, ROWS)], own_sem.at[0, c]
+        )
+        own.start()
+        dispatch.append((own, copies))
+
+    links = {}
+
+    def pair_send(kind, c, src, dst, peer):
+        links[kind, c] = remote(src, dst, pair_go.at[kind, c], pair_come.at[kind, c], peer)
+
+    def spread(c):
+        own, copies = dispatch[c]
+        own.wait()
+        for copy in copies:
+            copy.wait_recv()
+        pair_send(0, c, rows.at[c, 0], rows.at[c, 2], chip)
+        pair_send(1, c, rows.at[c, 0], rows.at[c, 1], core)
+
+    def relay(c):
+        links[0, c].wait_recv()
+        pair_send(2, c, rows.at[c, 2], rows.at[c, 3], core)
+
+    def compute(c):
+        e = c // per_expert
+        if c == 0:
+            for copy in w_copies:
+                copy.wait()
+        links[1, c].wait_recv()
+        links[2, c].wait_recv()
+        block = rows.shape[2]
+
+        def project_in(t, carry):
+            cols = pl.ds(pl.multiple_of(t * TILE, TILE), TILE)
+            x = rows[c].reshape(4 * block, rows.shape[3])
+            h = exact_dot(x, first[e, :, cols])
+            hidden[:, cols] = jnp.maximum(h, 0.0).astype(jnp.bfloat16)
+            return carry
+
+        lax.fori_loop(0, first.shape[2] // TILE, project_in, 0)
+
+        def project_out(t, carry):
+            cols = pl.ds(pl.multiple_of(t * TILE, TILE), TILE)
+            y = exact_dot(hidden[...], second[e, :, cols]).astype(jnp.bfloat16)
+            for k in range(4):
+                part[c, k, :, cols] = y[k * block : (k + 1) * block]
+            return carry
+
+        lax.fori_loop(0, second.shape[2] // TILE, project_out, 0)
+        pair_send(3, c, part.at[c, 3], near.at[c, 1], core)
+        pair_send(4, c, part.at[c, 1], near.at[c, 0], core)
+
+    def over_rows(body):
+        def step(t, carry):
+            body(pl.ds(pl.multiple_of(t * ROWS, ROWS), ROWS))
+            return carry
+
+        lax.fori_loop(0, n, step, 0)
+
+    def wide(x):
+        return x.astype(jnp.float32)
+
+    def cross(c):
+        links[3, c].wait_recv()
+
+        def add(r):
+            both = wide(part[c, 2, r, :]) + wide(near[c, 1, r, :])
+            part[c, 2, r, :] = both.astype(jnp.bfloat16)
+
+        over_rows(add)
+        pair_send(5, c, part.at[c, 2], far.at[c], chip)
+
+    def finish(c):
+        links[4, c].wait_recv()
+        links[5, c].wait_recv()
+
+        def add(r):
+            both = wide(part[c, 0, r, :]) + wide(near[c, 0, r, :]) + wide(far[c, r, :])
+            part[c, 0, r, :] = both.astype(jnp.bfloat16)
+
+        over_rows(add)
+        for j in range(1, n):
+            block = pl.ds(j * ROWS, ROWS)
+            sent.append(
+                remote(
+                    part.at[c, 0, block],
+                    back.at[c, block],
+                    go_sem.at[1, c, j],
+                    come_sem.at[1, c, j],
+                    behind[j],
+                )
+            )
+        own = pltpu.make_async_copy(
+            part.at[c, 0, pl.ds(0, ROWS)], back.at[c, pl.ds(0, ROWS)], own_sem.at[1, c]
+        )
+        own.start()
+        sent.append(own)
+
+    for i in range(chunks + 3):
+        if i < chunks:
+            spread(i)
+        if 0 <= i - 1 < chunks:
+            relay(i - 1)
+            compute(i - 1)
+        if 0 <= i - 2 < chunks:
+            cross(i - 2)
+        if 0 <= i - 3 < chunks:
+            finish(i - 3)
+
+    for _, copies in dispatch:
+        for copy in copies:
+            copy.wait_send()
+    for copy in links.values():
+        copy.wait_send()
+    for copy in sent:
+        copy.wait()
+
+
+def expert_layer(packed, w_in, w_out, n):
+    chunks, block, width = packed.shape
+    quarter = w_in.shape[2]
+    bf16 = jnp.bfloat16
+    dma = pltpu.SemaphoreType.DMA
+    anywhere = pl.BlockSpec(memory_space=pl.ANY)
+    return pl.pallas_call(
+        functools.partial(layer_kernel, n),
+        out_shape=jax.ShapeDtypeStruct(packed.shape, bf16),
+        in_specs=[anywhere] * 3,
+        out_specs=anywhere,
+        scratch_shapes=[
+            pltpu.VMEM(w_in.shape, bf16),
+            pltpu.VMEM(w_out.shape, bf16),
+            pltpu.VMEM((chunks, 4, block, width), bf16),
+            pltpu.VMEM((4 * block, quarter), bf16),
+            pltpu.VMEM((chunks, 4, block, width), bf16),
+            pltpu.VMEM((chunks, 2, block, width), bf16),
+            pltpu.VMEM((chunks, block, width), bf16),
+            dma((2, chunks)),
+            dma((2,)),
+            dma((2, chunks, n)),
+            dma((2, chunks, n)),
+            dma((6, chunks)),
+            dma((6, chunks)),
+        ],
+        compiler_params=pltpu.CompilerParams(
+            collective_id=0, has_side_effects=True, vmem_limit_bytes=60 * 1024 * 1024
+        ),
+    )(packed, w_in, w_out)
+
+
+def plain(tokens, token_ids, table, w_in, w_out):
     groups = lax.axis_size("expert")
     exp_local = w_in.shape[0]
     experts = groups * exp_local
@@ -53,6 +281,35 @@
     return jnp.dot(placer, flat, preferred_element_type=jnp.float32).astype(jnp.bfloat16)
 
 
+def on_device(tokens, token_ids, table, w_in, w_out):
+    n = lax.axis_size("expert")
+    me = lax.axis_index("expert")
+    exp_local = w_in.shape[0]
+    experts = n * exp_local
+    tok_rows, width = tokens.shape
+    slots = max(2, 2 * tok_rows // experts)
+    if slots % ROWS or lax.axis_size("pair") != 4:
+        return plain(tokens, token_ids, table, w_in, w_out)
+    per_expert = slots // ROWS
+
+    chosen = jnp.take(table, token_ids, axis=0)
+    hot = chosen[:, None] == jnp.arange(experts, dtype=jnp.int32)[None, :]
+    before = jnp.arange(tok_rows)[:, None] > jnp.arange(tok_rows)[None, :]
+    earlier = exact_dot(before.astype(jnp.bfloat16), hot.astype(jnp.bfloat16))
+    rank = jnp.sum(jnp.where(hot, earlier, 0.0), axis=1).astype(jnp.int32)
+    ahead = (chosen // exp_local - me + n) % n
+    chunk = chosen % exp_local * per_expert + rank // ROWS
+    column = jnp.where(rank < slots, (chunk * n + ahead) * ROWS + rank % ROWS, -1)
+
+    places = jnp.arange(experts * slots, dtype=jnp.int32)
+    placer = (places[:, None] == column[None, :]).astype(jnp.bfloat16)
+    packed = exact_dot(placer, tokens).astype(jnp.bfloat16)
+    packed = packed.reshape(exp_local * per_expert, n * ROWS, width)
+    back = expert_layer(packed, w_in, w_out, n).reshape(experts * slots, width)
+    picker = (column[:, None] == places[None, :]).astype(jnp.bfloat16)
+    return exact_dot(picker, back).astype(jnp.bfloat16)
+
+
 def solution(mesh):
     in_specs = (
         P(("expert", "pair"), None),

time: 338 us -> 196 us (0.58)
  Pallas kernels: 0 us -> 182 us
  blocking collectives: 154 us -> 0 us
  waiting for transfers between devices: 114 us -> 0 us
  matrix products: 34.6 us -> 8.13 us
  between operations: 13.5 us -> 0.03 us
  local copies, waits for them, and re-layouts: 16.6 us -> 3.44 us
    pallas_call x0 -> x1, Pallas kernels: none -> 182 us  [expert_layer(): pl.pallas_call(functools.partial(layer_kernel, n), out_shape=jax.ShapeDty...]
    all_to_all x2 -> x0, blocking collectives: 154 us -> none  [the longest x1 78 us: on_device(): lax.all_to_all(packed, 'expert', split_axis=0, concat_axis=0, tiled=True)]
    all_gather x2 -> x0, waiting for transfers between devices: 113 us -> none  [the longest x1 93.5 us: on_device(): piece = lax.all_gather(w_out, 'pair', axis=1, tiled=True)]
    dot_general x7 -> x3, matrix products: 34.6 us -> 8.13 us  [exact_dot(): return jnp.dot(a, b, preferred_element_type=jnp.float32)]
    reshape x2 -> x0, local copies, waits for them, and re-layouts: 10.6 us -> none  [the longest x1 5.83 us: on_device(): flat = returned.reshape(experts * slots, width)]
  transfers between devices with their start and end apart: 2 -> 0, of which waited for: 2 -> 0; matrix products, arithmetic and copies ran while one was open for 8% -> 0% of each run, Pallas kernels for 0% -> 0%
where the time goes in v1:
time: 196 us
  Pallas kernels  182 us (93%)
  matrix products  8.13 us (4%)
  local copies, waits for them, and re-layouts  3.44 us (2%)
    pallas_call x1, Pallas kernels, expert_layer(): pl.pallas_call(functools.partial(layer_kernel, n), out_shape=jax.ShapeDty...  182 us
    dot_general x3, matrix products, exact_dot(): return jnp.dot(a, b, preferred_element_type=jnp.float32)  8.13 us

profile of v1, /device:TPU:0, one launch (start us, length us, event | category | flops | bytes accessed | tf_op | source)
XLA Modules:
  0.0 195.5 jit_solution(9165975988396145569)
XLA Ops:
  0.0 0.0 copy-start
  0.0 0.8 compare_select_fusion
  0.8 3.4 %gather_fusion = s32[384]{0:T(512)S(1)} fusion(s32[8192]{0:T(1024)} %param.7, s32[1024]{0:T(1024)S(1)} %pad_clamp_fusion), kind=kCustom, calls=%fused_computation | custom fusion | bytes 4608 | tf_op jit(solution)/shard_map/jit(_take)/gather | solution.py:295
  4.3 0.7 and_select_fusion
  4.9 0.2 fusion
  5.2 0.0 copy-done
  5.2 3.5 %convolution_convert_fusion = bf16[768,2048]{1,0:T(8,128)(2,1)} fusion(bf16[384,2048]{1,0:T(8,128)(2,1)S(1)} %copy-done, s32[384]{0:T(512)S(1)} %fusion.10), kind=kOutput, calls=%fused_computation.1 | convolution fusion | flops 1209827328 | bytes 4720128 | tf_op jit(solution)/shard_map/dot_general | solution.py:16
  8.7 182.4 %shard_map.55 = bf16[6,128,2048]{2,1,0:T(8,128)(2,1)} custom-call(bf16[6,128,2048]{2,1,0:T(8,128)(2,1)} %bitcast.5, bf16[2,2048,512]{2,1,0:T(8,128)(2,1)} %w_in.1, bf16[2,512,2048]{2,1,0:T(8,128)(2,1)} %w_out.1), custom_call_target="tpu_custom_call" | custom-call | tf_op jit(solution)/shard_map/pallas_call | solution.py:209
  191.1 4.5 %convolution_convert_fusion.1 = bf16[384,2048]{1,0:T(8,128)(2,1)} fusion(bf16[768,2048]{1,0:T(8,128)(2,1)} %bitcast.4, s32[384]{0:T(512)S(1)} %fusion.10), kind=kOutput, calls=%fused_computation.2 | convolution fusion | flops 1209040896 | bytes 4720128 | tf_op jit(solution)/shard_map/dot_general | solution.py:16
  (2 shorter events, 0.0 us)
Async XLA Ops:
  0.0 5.2 %copy-start = (bf16[384,2048]{1,0:T(8,128)(2,1)S(1)}, bf16[384,2048]{1,0:T(8,128)(2,1)}, u32[]{:S(2)}) copy-start(bf16[384,2048]{1,0:T(8,128)(2,1)} %param.5) | copy-start | bytes 4718596

commit v2 on v1

--- a/solution.py
+++ b/solution.py
@@ -9,6 +9,8 @@
 
 ROWS = 16
 TILE = 256
+LAST_PIECES = 4
+LANES = 128
 MESH = pl.DeviceIdType.MESH
 
 
@@ -35,6 +37,11 @@
     come_sem,
     pair_go,
     pair_come,
+    part_go,
+    part_come,
+    ret_go,
+    ret_come,
+    ret_own,
 ):
     chunks = packed.shape[0]
     per_expert = chunks // w_in.shape[0]
@@ -71,47 +78,71 @@
 
     sent = []
     dispatch = []
-    for c in range(chunks):
-        copies = [
-            remote(
-                packed.at[c, pl.ds(j * ROWS, ROWS)],
-                rows.at[c, 0, pl.ds(j * ROWS, ROWS)],
-                go_sem.at[0, c, j],
-                come_sem.at[0, c, j],
-                ahead[j],
-            )
-            for j in range(1, n)
-        ]
-        own = pltpu.make_async_copy(
-            packed.at[c, pl.ds(0, ROWS)], rows.at[c, 0, pl.ds(0, ROWS)], own_sem.at[0, c]
-        )
-        own.start()
-        dispatch.append((own, copies))
-
     links = {}
 
     def pair_send(kind, c, src, dst, peer):
         links[kind, c] = remote(src, dst, pair_go.at[kind, c], pair_come.at[kind, c], peer)
 
+    def blocks(lo, hi):
+        return pl.ds(lo * ROWS, (hi - lo) * ROWS)
+
+    for c in range(chunks):
+        dispatch.append(
+            [
+                remote(
+                    packed.at[c, blocks(j, j + 1)],
+                    rows.at[c, 0, blocks(j, j + 1)],
+                    go_sem.at[c, j],
+                    come_sem.at[c, j],
+                    ahead[j],
+                )
+                for j in range(1, n)
+            ]
+        )
+    own_copies = []
+    for c in range(chunks):
+        own = blocks(0, 1)
+        pair_send(0, c, packed.at[c, own], rows.at[c, 2, own], chip)
+        pair_send(1, c, packed.at[c, own], rows.at[c, 1, own], core)
+        copy = pltpu.make_async_copy(packed.at[c, own], rows.at[c, 0, own], own_sem.at[c])
+        copy.start()
+        own_copies.append(copy)
+
+    groups = [(1, n // 2), (n // 2, n)]
+
     def spread(c):
-        own, copies = dispatch[c]
-        own.wait()
-        for copy in copies:
-            copy.wait_recv()
-        pair_send(0, c, rows.at[c, 0], rows.at[c, 2], chip)
-        pair_send(1, c, rows.at[c, 0], rows.at[c, 1], core)
+        for g, (lo, hi) in enumerate(groups):
+            for j in range(lo, hi):
+                dispatch[c][j - 1].wait_recv()
+            some = blocks(lo, hi)
+            pair_send(2 + 2 * g, c, rows.at[c, 0, some], rows.at[c, 2, some], chip)
+            pair_send(3 + 2 * g, c, rows.at[c, 0, some], rows.at[c, 1, some], core)
 
     def relay(c):
-        links[0, c].wait_recv()
-        pair_send(2, c, rows.at[c, 2], rows.at[c, 3], core)
+        for kind in (0, 2, 4):
+            links[kind, c].wait_recv()
+        pair_send(6, c, rows.at[c, 2], rows.at[c, 3], core)
+
+    def pieces(c):
+        return LAST_PIECES if c == chunks - 1 else 1
+
+    def columns(c, q):
+        size = part.shape[3] // pieces(c)
+        return pl.ds(q * size, size)
+
+    def part_send(kind, c, q, src, dst, peer):
+        links[kind, c, q] = remote(
+            src, dst, part_go.at[kind, c, q], part_come.at[kind, c, q], peer
+        )
 
     def compute(c):
         e = c // per_expert
         if c == 0:
             for copy in w_copies:
                 copy.wait()
-        links[1, c].wait_recv()
-        links[2, c].wait_recv()
+        own_copies[c].wait()
+        for kind in (1, 3, 5, 6):
+            links[kind, c].wait_recv()
         block = rows.shape[2]
 
         def project_in(t, carry):
@@ -130,9 +161,12 @@
                 part[c, k, :, cols] = y[k * block : (k + 1) * block]
             return carry
 
-        lax.fori_loop(0, second.shape[2] // TILE, project_out, 0)
-        pair_send(3, c, part.at[c, 3], near.at[c, 1], core)
-        pair_send(4, c, part.at[c, 1], near.at[c, 0], core)
+        steps = second.shape[2] // TILE // pieces(c)
+        for q in range(pieces(c)):
+            lax.fori_loop(q * steps, (q + 1) * steps, project_out, 0)
+            cols = columns(c, q)
+            part_send(0, c, q, part.at[c, 3, :, cols], near.at[c, 1, :, cols], core)
+            part_send(1, c, q, part.at[c, 1, :, cols], near.at[c, 0, :, cols], core)
 
     def over_rows(body):
         def step(t, carry):
@@ -145,40 +179,46 @@
         return x.astype(jnp.float32)
 
     def cross(c):
-        links[3, c].wait_recv()
-
-        def add(r):
-            both = wide(part[c, 2, r, :]) + wide(near[c, 1, r, :])
-            part[c, 2, r, :] = both.astype(jnp.bfloat16)
-
-        over_rows(add)
-        pair_send(5, c, part.at[c, 2], far.at[c], chip)
+        for q in range(pieces(c)):
+            links[0, c, q].wait_recv()
+            cols = columns(c, q)
+
+            def add(r):
+                both = wide(part[c, 2, r, cols]) + wide(near[c, 1, r, cols])
+                part[c, 2, r, cols] = both.astype(jnp.bfloat16)
+
+            over_rows(add)
+            part_send(2, c, q, part.at[c, 2, :, cols], far.at[c, :, cols], chip)
 
     def finish(c):
-        links[4, c].wait_recv()
-        links[5, c].wait_recv()
-
-        def add(r):
-            both = wide(part[c, 0, r, :]) + wide(near[c, 0, r, :]) + wide(far[c, r, :])
-            part[c, 0, r, :] = both.astype(jnp.bfloat16)
-
-        over_rows(add)
-        for j in range(1, n):
-            block = pl.ds(j * ROWS, ROWS)
-            sent.append(
-                remote(
-                    part.at[c, 0, block],
-                    back.at[c, block],
-                    go_sem.at[1, c, j],
-                    come_sem.at[1, c, j],
-                    behind[j],
+        for q in range(pieces(c)):
+            links[1, c, q].wait_recv()
+            links[2, c, q].wait_recv()
+            cols = columns(c, q)
+
+            def add(r):
+                both = wide(part[c, 0, r, cols]) + wide(near[c, 0, r, cols])
+                both = both + wide(far[c, r, cols])
+                part[c, 0, r, cols] = both.astype(jnp.bfloat16)
+
+            over_rows(add)
+            for j in range(1, n):
+                some = blocks(j, j + 1)
+                sent.append(
+                    remote(
+                        part.at[c, 0, some, cols],
+                        back.at[c, some, cols],
+                        ret_go.at[c, q, j],
+                        ret_come.at[c, q, j],
+                        behind[j],
+                    )
                 )
+            own = blocks(0, 1)
+            copy = pltpu.make_async_copy(
+                part.at[c, 0, own, cols], back.at[c, own, cols], ret_own.at[c, q]
             )
-        own = pltpu.make_async_copy(
-            part.at[c, 0, pl.ds(0, ROWS)], back.at[c, pl.ds(0, ROWS)], own_sem.at[1, c]
-        )
-        own.start()
-        sent.append(own)
+            copy.start()
+            sent.append(copy)
 
     for i in range(chunks + 3):
         if i < chunks:
@@ -191,13 +231,21 @@
         if 0 <= i - 3 < chunks:
             finish(i - 3)
 
-    for _, copies in dispatch:
+    for copies in dispatch:
         for copy in copies:
             copy.wait_send()
     for copy in links.values():
         copy.wait_send()
     for copy in sent:
         copy.wait()
+
+
+def look_up(table, ids):
+    lines = table.reshape(-1, LANES).astype(jnp.bfloat16)
+    line = ids[:, None] // LANES == jnp.arange(lines.shape[0], dtype=jnp.int32)[None, :]
+    found = exact_dot(line.astype(jnp.bfloat16), lines)
+    lane = ids[:, None] % LANES == jnp.arange(LANES, dtype=jnp.int32)[None, :]
+    return jnp.sum(jnp.where(lane, found, 0.0), axis=1).astype(jnp.int32)
 
 
 def expert_layer(packed, w_in, w_out, n):
@@ -219,12 +267,17 @@
             pltpu.VMEM((chunks, 4, block, width), bf16),
             pltpu.VMEM((chunks, 2, block, width), bf16),
             pltpu.VMEM((chunks, block, width), bf16),
-            dma((2, chunks)),
+            dma((chunks,)),
             dma((2,)),
-            dma((2, chunks, n)),
-            dma((2, chunks, n)),
-            dma((6, chunks)),
-            dma((6, chunks)),
+            dma((chunks, n)),
+            dma((chunks, n)),
+            dma((7, chunks)),
+            dma((7, chunks)),
+            dma((3, chunks, LAST_PIECES)),
+            dma((3, chunks, LAST_PIECES)),
+            dma((chunks, LAST_PIECES, n)),
+            dma((chunks, LAST_PIECES, n)),
+            dma((chunks, LAST_PIECES)),
         ],
         compiler_params=pltpu.CompilerParams(
             collective_id=0, has_side_effects=True, vmem_limit_bytes=60 * 1024 * 1024
@@ -288,11 +341,11 @@
     experts = n * exp_local
     tok_rows, width = tokens.shape
     slots = max(2, 2 * tok_rows // experts)
-    if slots % ROWS or lax.axis_size("pair") != 4:
+    if slots % ROWS or table.shape[0] % LANES or lax.axis_size("pair") != 4 or experts > 256:
         return plain(tokens, token_ids, table, w_in, w_out)
     per_expert = slots // ROWS
 
-    chosen = jnp.take(table, token_ids, axis=0)
+    chosen = look_up(table, token_ids)
     hot = chosen[:, None] == jnp.arange(experts, dtype=jnp.int32)[None, :]
     before = jnp.arange(tok_rows)[:, None] > jnp.arange(tok_rows)[None, :]
     earlier = exact_dot(before.astype(jnp.bfloat16), hot.astype(jnp.bfloat16))

time: 196 us -> 186 us (0.949)
  Pallas kernels: 182 us -> 176 us
  local copies, waits for them, and re-layouts: 3.44 us -> 0.01 us
    pallas_call x1, Pallas kernels: 182 us -> 176 us  [expert_layer(): pl.pallas_call(functools.partial(layer_kernel, n), out_shape=jax.ShapeDty...]
    gather x1 -> x0, local copies, waits for them, and re-layouts: 3.44 us -> none  [on_device(): chosen = jnp.take(table, token_ids, axis=0)]
    dot_general x3 -> x4, matrix products: 8.13 us -> 9.17 us  [exact_dot(): return jnp.dot(a, b, preferred_element_type=jnp.float32)]
where the time goes in v2:
time: 186 us
  Pallas kernels  176 us (95%)
  matrix products  9.17 us (5%)
    pallas_call x1, Pallas kernels, expert_layer(): pl.pallas_call(functools.partial(layer_kernel, n), out_shape=jax.ShapeDty...  176 us
    dot_general x4, matrix products, exact_dot(): return jnp.dot(a, b, preferred_element_type=jnp.float32)  9.17 us

profile of v2, /device:TPU:0, one launch (start us, length us, event | category | flops | bytes accessed | tf_op | source)
XLA Modules:
  0.0 186.0 jit_solution(2207856552961930711)
XLA Ops:
  0.0 0.0 copy-start
  0.0 0.8 add_select_fusion.6
  0.8 1.1 fusion
  1.9 0.2 fusion.1
  2.1 0.0 copy-done
  2.1 3.5 %convolution_convert_fusion = bf16[768,2048]{1,0:T(8,128)(2,1)} fusion(bf16[384,2048]{1,0:T(8,128)(2,1)S(1)} %copy-done, s32[384]{0:T(512)S(1)} %fusion.14), kind=kOutput, calls=%fused_computation | convolution fusion | flops 1209827328 | bytes 4720128 | tf_op jit(solution)/shard_map/dot_general | solution.py:18
  5.6 176.0 %shard_map.55 = bf16[6,128,2048]{2,1,0:T(8,128)(2,1)} custom-call(bf16[6,128,2048]{2,1,0:T(8,128)(2,1)} %bitcast.8, bf16[2,2048,512]{2,1,0:T(8,128)(2,1)} %w_in.1, bf16[2,512,2048]{2,1,0:T(8,128)(2,1)} %w_out.1), custom_call_target="tpu_custom_call" | custom-call | tf_op jit(solution)/shard_map/pallas_call | solution.py:257
  181.6 4.5 %convolution_convert_fusion.1 = bf16[384,2048]{1,0:T(8,128)(2,1)} fusion(bf16[768,2048]{1,0:T(8,128)(2,1)} %bitcast.7, s32[384]{0:T(512)S(1)} %fusion.14), kind=kOutput, calls=%fused_computation.1 | convolution fusion | flops 1209040896 | bytes 4720128 | tf_op jit(solution)/shard_map/dot_general | solution.py:18
  (2 shorter events, 0.0 us)
Async XLA Ops:
  0.0 2.1 %copy-start = (bf16[384,2048]{1,0:T(8,128)(2,1)S(1)}, bf16[384,2048]{1,0:T(8,128)(2,1)}, u32[]{:S(2)}) copy-start(bf16[384,2048]{1,0:T(8,128)(2,1)} %param.5) | copy-start | bytes 4718596

commit v3 on v2

--- a/solution.py
+++ b/solution.py
@@ -16,6 +16,21 @@
 
 def exact_dot(a, b):
     return jnp.dot(a, b, preferred_element_type=jnp.float32)
+
+
+def across(me, j):
+    other = me
+    bit = 1
+    while bit <= j:
+        if j & bit:
+            other = other + bit * (1 - 2 * (me // bit % 2))
+        bit *= 2
+    return other
+
+
+def send_order(chunks, n):
+    first = [(c, 1) for c in range(chunks)]
+    return first + [(c, j) for c in range(chunks) for j in range(2, n)]
 
 
 def layer_kernel(
@@ -49,8 +64,7 @@
     at = lax.axis_index("pair")
     core = {"pair": at + 1 - 2 * (at % 2)}
     chip = {"pair": (at + 2) % 4}
-    ahead = [{"expert": (me + j) % n} for j in range(n)]
-    behind = [{"expert": (me + n - j) % n} for j in range(n)]
+    ahead = [{"expert": across(me, j)} for j in range(n)]
 
     w_copies = [
         pltpu.make_async_copy(w_in, first, w_sem.at[0]),
@@ -77,7 +91,7 @@
         return copy
 
     sent = []
-    dispatch = []
+    dispatch = {}
     links = {}
 
     def pair_send(kind, c, src, dst, peer):
@@ -86,19 +100,17 @@
     def blocks(lo, hi):
         return pl.ds(lo * ROWS, (hi - lo) * ROWS)
 
-    for c in range(chunks):
-        dispatch.append(
-            [
-                remote(
-                    packed.at[c, blocks(j, j + 1)],
-                    rows.at[c, 0, blocks(j, j + 1)],
-                    go_sem.at[c, j],
-                    come_sem.at[c, j],
-                    ahead[j],
-                )
-                for j in range(1, n)
-            ]
+    def send_block(c, j):
+        dispatch[c, j] = remote(
+            packed.at[c, blocks(j, j + 1)],
+            rows.at[c, 0, blocks(j, j + 1)],
+            go_sem.at[c, j],
+            come_sem.at[c, j],
+            ahead[j],
         )
+
+    for c, j in send_order(chunks, n):
+        send_block(c, j)
     own_copies = []
     for c in range(chunks):
         own = blocks(0, 1)
@@ -108,20 +120,20 @@
         copy.start()
         own_copies.append(copy)
 
-    groups = [(1, n // 2), (n // 2, n)]
-
-    def spread(c):
-        for g, (lo, hi) in enumerate(groups):
-            for j in range(lo, hi):
-                dispatch[c][j - 1].wait_recv()
-            some = blocks(lo, hi)
-            pair_send(2 + 2 * g, c, rows.at[c, 0, some], rows.at[c, 2, some], chip)
-            pair_send(3 + 2 * g, c, rows.at[c, 0, some], rows.at[c, 1, some], core)
+    groups = [(1, 2), (2, n // 2), (n // 2, n)]
+
+    def spread(c, g):
+        lo, hi = groups[g]
+        for j in range(lo, hi):
+            dispatch[c, j].wait_recv()
+        some = blocks(lo, hi)
+        pair_send(2 + 2 * g, c, rows.at[c, 0, some], rows.at[c, 2, some], chip)
+        pair_send(3 + 2 * g, c, rows.at[c, 0, some], rows.at[c, 1, some], core)
 
     def relay(c):
-        for kind in (0, 2, 4):
+        for kind in (0, 2, 4, 6):
             links[kind, c].wait_recv()
-        pair_send(6, c, rows.at[c, 2], rows.at[c, 3], core)
+        pair_send(8, c, rows.at[c, 2], rows.at[c, 3], core)
 
     def pieces(c):
         return LAST_PIECES if c == chunks - 1 else 1
@@ -141,7 +153,7 @@
             for copy in w_copies:
                 copy.wait()
         own_copies[c].wait()
-        for kind in (1, 3, 5, 6):
+        for kind in (1, 3, 5, 7, 8):
             links[kind, c].wait_recv()
         block = rows.shape[2]
 
@@ -210,7 +222,7 @@
                         back.at[c, some, cols],
                         ret_go.at[c, q, j],
                         ret_come.at[c, q, j],
-                        behind[j],
+                        ahead[j],
                     )
                 )
             own = blocks(0, 1)
@@ -220,20 +232,23 @@
             copy.start()
             sent.append(copy)
 
+    def spread0(c):
+        spread(c, 1)
+
+    def spread1(c):
+        spread(c, 2)
+
+    for c in range(chunks):
+        spread(c, 0)
+
+    order = [(spread0, 0), (relay, 1), (spread1, 0), (compute, 1), (cross, 1), (finish, 2)]
     for i in range(chunks + 3):
-        if i < chunks:
-            spread(i)
-        if 0 <= i - 1 < chunks:
-            relay(i - 1)
-            compute(i - 1)
-        if 0 <= i - 2 < chunks:
-            cross(i - 2)
-        if 0 <= i - 3 < chunks:
-            finish(i - 3)
-
-    for copies in dispatch:
-        for copy in copies:
-            copy.wait_send()
+        for stage, late in order:
+            if 0 <= i - late < chunks:
+                stage(i - late)
+
+    for copy in dispatch.values():
+        copy.wait_send()
     for copy in links.values():
         copy.wait_send()
     for copy in sent:
@@ -271,8 +286,8 @@
             dma((2,)),
             dma((chunks, n)),
             dma((chunks, n)),
-            dma((7, chunks)),
-            dma((7, chunks)),
+            dma((9, chunks)),
+            dma((9, chunks)),
             dma((3, chunks, LAST_PIECES)),
             dma((3, chunks, LAST_PIECES)),
             dma((chunks, LAST_PIECES, n)),
@@ -341,7 +356,7 @@
     experts = n * exp_local
     tok_rows, width = tokens.shape
     slots = max(2, 2 * tok_rows // experts)
-    if slots % ROWS or table.shape[0] % LANES or lax.axis_size("pair") != 4 or experts > 256:
+    if slots % ROWS or table.shape[0] % LANES or lax.axis_size("pair") != 4 or experts > 256 or n < 8 or n & (n - 1):
         return plain(tokens, token_ids, table, w_in, w_out)
     per_expert = slots // ROWS
 
@@ -350,7 +365,7 @@
     before = jnp.arange(tok_rows)[:, None] > jnp.arange(tok_rows)[None, :]
     earlier = exact_dot(before.astype(jnp.bfloat16), hot.astype(jnp.bfloat16))
     rank = jnp.sum(jnp.where(hot, earlier, 0.0), axis=1).astype(jnp.int32)
-    ahead = (chosen // exp_local - me + n) % n
+    ahead = jnp.bitwise_xor(chosen // exp_local, me)
     chunk = chosen % exp_local * per_expert + rank // ROWS
     column = jnp.where(rank < slots, (chunk * n + ahead) * ROWS + rank % ROWS, -1)
 

time: 186 us -> 174 us (0.935)
  Pallas kernels: 176 us -> 163 us
    pallas_call x1, Pallas kernels: 176 us -> 163 us  [expert_layer(): pl.pallas_call(functools.partial(layer_kernel, n), out_shape=jax.ShapeDty...]
where the time goes in v3:
time: 174 us; the launch traced here: 173 us
  Pallas kernels  163 us (94%)
  matrix products  9.18 us (5%)
    pallas_call x1, Pallas kernels, expert_layer(): pl.pallas_call(functools.partial(layer_kernel, n), out_shape=jax.ShapeDty...  163 us
    dot_general x4, matrix products, exact_dot(): return jnp.dot(a, b, preferred_element_type=jnp.float32)  9.18 us

profile of v3, /device:TPU:0, one launch (start us, length us, event | category | flops | bytes accessed | tf_op | source)
XLA Modules:
  0.0 173.2 jit_solution(6394004169689579199)
XLA Ops:
  0.0 0.0 copy-start
  0.0 0.8 add_select_fusion.5
  0.8 1.1 fusion
  1.9 0.2 fusion.1
  2.1 0.0 copy-done
  2.1 3.5 %convolution_convert_fusion = bf16[768,2048]{1,0:T(8,128)(2,1)} fusion(bf16[384,2048]{1,0:T(8,128)(2,1)S(1)} %copy-done, s32[384]{0:T(512)S(1)} %fusion.14), kind=kOutput, calls=%fused_computation | convolution fusion | flops 1209827328 | bytes 4720128 | tf_op jit(solution)/shard_map/dot_general | solution.py:18
  5.6 163.1 %shard_map.55 = bf16[6,128,2048]{2,1,0:T(8,128)(2,1)} custom-call(bf16[6,128,2048]{2,1,0:T(8,128)(2,1)} %bitcast.8, bf16[2,2048,512]{2,1,0:T(8,128)(2,1)} %w_in.1, bf16[2,512,2048]{2,1,0:T(8,128)(2,1)} %w_out.1), custom_call_target="tpu_custom_call" | custom-call | tf_op jit(solution)/shard_map/pallas_call | solution.py:272
  168.7 4.5 %convolution_convert_fusion.1 = bf16[384,2048]{1,0:T(8,128)(2,1)} fusion(bf16[768,2048]{1,0:T(8,128)(2,1)} %bitcast.7, s32[384]{0:T(512)S(1)} %fusion.14), kind=kOutput, calls=%fused_computation.1 | convolution fusion | flops 1209040896 | bytes 4720128 | tf_op jit(solution)/shard_map/dot_general | solution.py:18
  (2 shorter events, 0.0 us)
Async XLA Ops:
  0.0 2.1 %copy-start = (bf16[384,2048]{1,0:T(8,128)(2,1)S(1)}, bf16[384,2048]{1,0:T(8,128)(2,1)}, u32[]{:S(2)}) copy-start(bf16[384,2048]{1,0:T(8,128)(2,1)} %param.5) | copy-start | bytes 4718596
